TPU v7x, 256 devices: a whole 4x4x8 slice. The times are simulated.
256 devices in a mesh: row: 16 (over x_hi, z), col: 16 (over x_lo, y, core).
Axes of the slice: x: 4 (x_hi: 2, x_lo: 2; x = x_hi * 2 + x_lo), y: 4, z: 8, core: 2. Of those that a mesh axis runs over, the one named last changes fastest.
Arguments:
- pair: bfloat16 [512, 512, 128], P('row', 'col'), may hold values from -6 to 6
- norm_in: float32 [128], replicated, may hold values from 0.1 to 1.9
- shift_in: float32 [128], replicated, may hold values from -3 to 3
- in_weight: bfloat16 [128, 640], replicated, may hold values from -0.5 to 0.5
- norm_out: float32 [128], replicated, may hold values from 0.1 to 1.9
- shift_out: float32 [128], replicated, may hold values from -3 to 3
- out_weight: bfloat16 [128, 128], replicated, may hold values from -0.5 to 0.5
Outputs:
- update: bfloat16 [512, 512, 128], P('row', 'col')
All inputs are finite; a program needn't handle non-finite values.
Results may differ from a plain program's by a relative error of at most 0.0054.
Values may be sent and summed in bfloat16 or wider, within the bound.
A program may use at most 64 MiB of HBM per device.

v0:
```python
import jax
import jax.numpy as jnp
from jax import lax
from jax.sharding import PartitionSpec as P

EPSILON = 1e-05


def layer_norm(values, gain, shift):
    values = values.astype(jnp.float32)
    center = jnp.mean(values, axis=-1, keepdims=True)
    spread = jnp.mean(jnp.square(values - center), axis=-1, keepdims=True)
    return (values - center) * lax.rsqrt(spread + EPSILON) * gain + shift


def local(pair, norm_in, shift_in, in_weight, norm_out, shift_out, out_weight):
    row_count, col_count, channels = pair.shape
    hidden = out_weight.shape[0]
    normed = layer_norm(pair, norm_in, shift_in).astype(jnp.bfloat16)
    projected = jnp.dot(normed.reshape(-1, channels), in_weight, preferred_element_type=jnp.float32)
    left = (jax.nn.sigmoid(projected[:, :hidden]) * projected[:, hidden : 2 * hidden]).astype(
        jnp.bfloat16
    )
    right = (
        jax.nn.sigmoid(projected[:, 2 * hidden : 3 * hidden])
        * projected[:, 3 * hidden : 4 * hidden]
    ).astype(jnp.bfloat16)
    gate = jax.nn.sigmoid(projected[:, 4 * hidden :]).reshape(row_count, col_count, channels)
    left = left.reshape(row_count, col_count, hidden)
    right = right.reshape(row_count, col_count, hidden)
    row_devices = lax.axis_size("row")
    col_devices = lax.axis_size("col")
    unit = row_count // col_devices
    groups = row_devices // col_devices
    sectioned = left.reshape(row_count, groups, col_devices, unit, hidden).transpose(0, 2, 1, 3, 4)
    sorted_parts = lax.all_to_all(sectioned, "col", split_axis=1, concat_axis=1, tiled=True)
    sorted_parts = sorted_parts.reshape(row_count, row_devices, unit * hidden)
    own_parts = lax.all_to_all(sorted_parts, "row", split_axis=1, concat_axis=0, tiled=True)
    own_parts = own_parts.reshape(row_count * row_devices, unit, hidden)
    right_full = lax.all_gather(right, "row", axis=0, tiled=True)
    mixed = jnp.einsum(
        "kih,kjh->ijh",
        lax.all_gather(own_parts, "col", axis=1, tiled=True),
        right_full,
        preferred_element_type=jnp.float32,
    )
    mixed_normed = layer_norm(mixed, norm_out, shift_out).astype(jnp.bfloat16)
    outward = jnp.dot(
        mixed_normed.reshape(-1, hidden), out_weight, preferred_element_type=jnp.float32
    )
    return (gate * outward.reshape(row_count, col_count, channels)).astype(jnp.bfloat16)


def solution(mesh):
    in_specs = (P("row", "col", None), P(), P(), P(), P(), P(), P())
    out_specs = P("row", "col", None)
    return jax.shard_map(local, mesh=mesh, in_specs=in_specs, out_specs=out_specs, check_vma=False)
```

profile of v0, /device:TPU:3, one launch (start us, length us, event | category | flops | bytes accessed | tf_op | source)
XLA Modules:
  0.0 178.1 jit_solution(12223654991282901006)
XLA Ops:
  6.5 0.0 copy-start
  6.5 0.0 all-gather.3.cloned.1.call-start
  6.5 1.2 convert_reduce_fusion
  7.8 1.3 fusion.3
  9.1 1.3 fusion.6
  10.4 0.0 copy-done
  10.4 0.5 fusion.23
  10.9 1.1 fusion.7
  12.0 0.0 all-gather.3.cloned.1.call-update
  12.1 0.0 all-gather.5.cloned.1.call-start
  12.1 0.2 copy.34
  12.4 12.6 %all_to_all.20 = bf16[32,16,1,2,128]{4,3,0,2,1:T(2,128)(2,1)S(1)} all-to-all(bf16[32,16,1,2,128]{4,3,0,2,1:T(2,128)(2,1)S(1)} %copy.34), channel_id=1, replica_groups=mesh['row'=16,'col'=16] {'col'}, dimensions={1} | all-to-all | bytes 524288 | tf_op jit(solution)/shard_map/all_to_all | solution.py:36
  25.0 0.2 reshape.51
  25.1 23.1 %all_to_all.21 = bf16[32,16,256]{2,0,1:T(8,128)(2,1)S(1)} all-to-all(bf16[32,16,256]{2,0,1:T(8,128)(2,1)S(1)} %reshape.51), channel_id=1, replica_groups=mesh['row'=16,'col'=16] {'row'}, dimensions={1} | all-to-all | bytes 524288 | tf_op jit(solution)/shard_map/all_to_all | solution.py:38
  48.2 0.1 reshape.52
  48.3 0.7 copy.35
  49.1 0.0 all-gather.5.cloned.1.call-update
  49.1 63.6 %all-gather.3.cloned.1.call-done = bf16[512,32,128]{2,1,0:T(8,128)(2,1)} async-done(((bf16[32,32,128]{2,1,0:T(8,128)(2,1)}), bf16[512,32,128]{2,1,0:T(8,128)(2,1)}) %all-gather.3.cloned.1.call-update) | async-done | bytes 4194320 | tf_op jit(solution)/shard_map/all_gather | solution.py:40
  112.7 8.6 %copy.36 = bf16[512,32,128]{0,1,2:T(8,128)(2,1)} copy(bf16[512,32,128]{2,1,0:T(8,128)(2,1)} %all-gather.3.cloned.1.call-done) | data formatting | bytes 8388608 | tf_op jit(solution)/shard_map/all_gather | solution.py:40
  121.3 34.2 %all-gather.5.cloned.1.call-done = bf16[512,32,128]{2,0,1:T(8,128)(2,1)} async-done(((bf16[512,2,128]{2,0,1:T(8,128)(2,1)}), bf16[512,32,128]{2,0,1:T(8,128)(2,1)}) %all-gather.5.cloned.1.call-update) | async-done | bytes 4194320 | tf_op jit(solution)/shard_map/all_gather | solution.py:43
  155.5 7.9 %copy.37 = bf16[512,32,128]{0,1,2:T(8,128)(2,1)} copy(bf16[512,32,128]{2,0,1:T(8,128)(2,1)} %all-gather.5.cloned.1.call-done) | data formatting | bytes 8388608 | tf_op jit(solution)/shard_map/all_gather | solution.py:43
  163.4 0.0 copy-start.1
  163.4 0.0 copy-start.2
  163.5 0.0 copy-start.3
  163.5 4.7 %bitcast_reduce_fusion = (f32[32,32]{0,1:T(8,128)S(1)}, f32[128,32,32]{2,1,0:T(8,128)S(1)}) fusion(bf16[512,32,128]{0,1,2:T(8,128)(2,1)} %copy.36, bf16[512,32,128]{0,1,2:T(8,128)(2,1)} %copy.37), kind=kOutput, calls=%fused_computation | convolution fusion | flops 134347776 | bytes 8916992 | tf_op jit(solution)/shard_map/kih,kjh->ijh/dot_general | solution.py:41
  168.2 0.1 copy.40
  168.3 1.4 copy.38
  169.7 0.4 multiply_reduce_fusion
  170.1 0.0 copy-done.1
  170.1 0.0 copy-done.2
  170.1 0.0 copy-done.3
  170.1 1.2 fusion
  (4 shorter events, 0.0 us)
Async XLA Ops:
  6.5 3.9 %copy-start = (bf16[128,640]{1,0:T(8,128)(2,1)S(1)}, bf16[128,640]{1,0:T(8,128)(2,1)}, u32[]{:S(2)}) copy-start(bf16[128,640]{1,0:T(8,128)(2,1)} %param.10) | copy-start | bytes 491524
  6.5 106.1 %all-gather.3.cloned.1.call-start = ((), (), s32[]{:S(2)}) async-start(), calls=%async_computation.2 | async-start | bytes 4456448 | tf_op jit(solution)/shard_map/all_gather | solution.py:40
  12.1 143.5 %all-gather.5.cloned.1.call-start = ((), (), s32[]{:S(2)}) async-start(), calls=%async_computation.3 | async-start | bytes 4456448 | tf_op jit(solution)/shard_map/all_gather | solution.py:43
  163.4 6.6 %copy-start.1 = (bf16[128,128]{1,0:T(8,128)(2,1)S(1)}, bf16[128,128]{1,0:T(8,128)(2,1)}, u32[]{:S(2)}) copy-start(bf16[128,128]{1,0:T(8,128)(2,1)} %param.13) | copy-start | bytes 98308
  163.4 6.7 %copy-start.2 = (f32[128]{0:T(128)S(1)}, f32[128]{0:T(128)}, u32[]{:S(2)}) copy-start(f32[128]{0:T(128)} %param.12) | copy-start | bytes 1540
  163.5 6.7 %copy-start.3 = (f32[128]{0:T(128)S(1)}, f32[128]{0:T(128)}, u32[]{:S(2)}) copy-start(f32[128]{0:T(128)} %param.11) | copy-start | bytes 1540
Sparse Core Ops, SparseCore 0:
  12.2 100.4 all-gather.2
  114.5 40.9 all-gather.4
where the time goes:
time: 180 us; the launch traced here: 178 us
  waiting for transfers between devices  97.8 us (54%)
  blocking collectives  35.7 us (20%)
  local copies, waits for them, and re-layouts  19.3 us (11%)
  between operations  13.5 us (8%)
  matrix products  6.37 us (4%)
  other arithmetic  5.36 us (3%)
    all_gather x1, waiting for transfers between devices, local(): right_full = lax.all_gather(right, 'row', axis=0, tiled=True)  63.6 us
    all_gather x1, waiting for transfers between devices, local(): lax.all_gather(own_parts, 'col', axis=1, tiled=True)  34.2 us
    all_to_all x1, blocking collectives, local(): lax.all_to_all(sorted_parts, 'row', split_axis=1, concat_axis=0, tiled=True)  23.1 us
    all_to_all x1, blocking collectives, local(): lax.all_to_all(sectioned, 'col', split_axis=1, concat_axis=1, tiled=True)  12.6 us
    all_gather x1, local copies, waits for them, and re-layouts, local(): right_full = lax.all_gather(right, 'row', axis=0, tiled=True)  8.62 us
    all_gather x1, local copies, waits for them, and re-layouts, local(): lax.all_gather(own_parts, 'col', axis=1, tiled=True)  7.93 us
    dot_general x1, matrix products, local(): jnp.einsum('kih,kjh->ijh', lax.all_gather(own_parts, 'col', axis=1, tiled...  4.72 us
  transfers between devices with their start and end apart: 2, of which 2 were waited for; matrix products, arithmetic and copies ran while one was open for 6% of the time, Pallas kernels for 0%

commit v1 on v0

v1 whole, which is shorter than its diff:
```python
import jax
import jax.numpy as jnp
from jax import lax
from jax.experimental import pallas as pl
from jax.experimental.pallas import tpu as pltpu
from jax.sharding import PartitionSpec as P

EPSILON = 1e-05
MESH = pl.DeviceIdType.MESH
PITCH = 40
NT = (((1,), (1,)), ((), ()))
TN = (((0,), (0,)), ((), ()))


def z_step(t):
    return 4 + (1 - 2 * (t % 2)) * ((t + 1) // 2)


def y_step(u):
    return 2 + (1 - 2 * lax.rem(u, 2)) * lax.div(u + 1, 2)


def swap_blocks(tiles):
    lane = lax.broadcasted_iota(jnp.int32, tiles[0].shape, 1)
    low, even = lane < 64, lax.rem(lax.div(lane, 32), 2) == 0

    def turn(x, shift):
        return pltpu.roll(x, shift, 1)

    a, b, c, d = tiles
    a, c = jnp.where(low, a, turn(c, 64)), jnp.where(low, turn(a, 64), c)
    b, d = jnp.where(low, b, turn(d, 64)), jnp.where(low, turn(b, 64), d)
    a, b = jnp.where(even, a, turn(b, 32)), jnp.where(even, turn(a, 96), b)
    c, d = jnp.where(even, c, turn(d, 32)), jnp.where(even, turn(c, 96), d)
    return a, b, c, d


def kernel(
    pair, norm_in, shift_in, in_weight, norm_out, shift_out, out_weight, out,
    normed, staged, sent, landed, left, right, mixed, back, gate, gain, bias, weight,
    dma, ready,
):
    f32, bf16 = jnp.float32, jnp.bfloat16
    r, c = lax.axis_index("row"), lax.axis_index("col")
    xh, z = lax.div(r, 8), lax.rem(r, 8)
    xl, y, core = lax.div(c, 8), lax.rem(lax.div(c, 2), 4), lax.rem(c, 2)
    spot = lax.div(c, 2)

    barrier = pltpu.get_barrier_semaphore()
    for s in range(1, 16):
        pl.semaphore_signal(barrier, inc=1, device_id=(lax.rem(r + s, 16), c), device_id_type=MESH)
    for s in range(1, 16):
        pl.semaphore_signal(barrier, inc=1, device_id=(r, lax.rem(c + s, 16)), device_id_type=MESH)

    def norm_rows(n, _):
        x = pair[pl.ds(n * 128, 128), :].astype(f32)
        center = jnp.mean(x, axis=-1, keepdims=True)
        x = x - center
        spread = jnp.mean(x * x, axis=-1, keepdims=True)
        x = x * lax.rsqrt(spread + EPSILON) * norm_in[...] + shift_in[...]
        for m in range(4):
            normed[pl.ds((n * 4 + m) * PITCH, 32), :] = x[m * 32 : (m + 1) * 32]
        return 0

    lax.fori_loop(0, 8, norm_rows, 0)
    weight[...] = in_weight[:, :512].astype(f32).T.astype(bf16)

    def glu(rows, x):
        p = lax.dot_general(weight[pl.ds(rows, 256), :], x, NT, preferred_element_type=f32)
        return jax.nn.sigmoid(p[:128]) * p[128:]

    for s in range(0, 8, 2):
        parts = [normed[pl.ds(b * 8 + s + e, 32, stride=PITCH), :] for e in range(2) for b in range(4)]
        value = glu(0, jnp.concatenate(parts, axis=0).astype(bf16))
        for e in range(2):
            staged[pl.ds(s + e, 128, stride=16), :] = value[:, e * 128 : (e + 1) * 128]
        parts = [normed[pl.ds((b * 8 + s + e) * PITCH, 32), :] for e in range(2) for b in range(4)]
        value = glu(256, jnp.concatenate(parts, axis=0).astype(bf16))
        for e in range(2):
            staged[pl.ds(8 + s + e, 128, stride=16), :] = value[:, e * 128 : (e + 1) * 128]

    def pack(n, _):
        sent[pl.ds(n * 16, 16)] = staged[pl.ds(n * 256, 256), :].astype(bf16).reshape(16, 16, 128)
        return 0

    lax.fori_loop(0, 8, pack, 0)

    pl.semaphore_wait(barrier, 30)
    for s in range(1, 16):
        pl.semaphore_signal(ready, inc=1, device_id=(r, lax.rem(c + s, 16)), device_id_type=MESH)
    pl.semaphore_wait(ready, 15)

    def inward(R, S, send):
        return pltpu.make_async_remote_copy(
            src_ref=sent.at[R * 8 + S], dst_ref=landed.at[r, lax.rem(c, 8)], send_sem=dma.at[send],
            recv_sem=dma.at[1], device_id=(R, S * 2 + xl), device_id_type=MESH,
        )

    for t in range(8):
        def go_in(s, _, t=t):
            R = lax.rem(xh + 1 - lax.div(s, 8), 2) * 8 + lax.rem(z + z_step(t), 8)
            S = lax.rem(xl + 1 - lax.rem(lax.div(s, 4), 2), 2) * 4 + lax.rem(y + y_step(lax.rem(s, 4)), 4)
            inward(R, S, 0).start()
            return 0

        lax.fori_loop(0, 16 if t < 7 else 15, go_in, 0)
    own_in = pltpu.make_async_copy(sent.at[r * 8 + spot], landed.at[r, lax.rem(c, 8)], dma.at[1])
    pl.when(xl == core)(own_in.start)
    pl.when(xl != core)(inward(r, spot, 2).start)

    def gate_rows(n, _):
        parts = [normed[pl.ds((n * 4 + m) * PITCH, 32), :] for m in range(4)]
        x = jnp.concatenate(parts, axis=0).astype(bf16)
        p = jnp.dot(x, in_weight[:, 512:], preferred_element_type=f32)
        gate[pl.ds(n * 4, 4)] = jax.nn.sigmoid(p).reshape(4, 32, 128)
        return 0

    lax.fori_loop(0, 8, gate_rows, 0)
    gain[...] = jnp.broadcast_to(norm_out[...], (128, 128)).T
    bias[...] = jnp.broadcast_to(shift_out[...], (128, 128)).T

    pltpu.make_async_copy(landed, landed, dma.at[1]).wait()

    for q in range(2):
        tiles = [landed[:, q * 4 + n].astype(f32)[:, 8:].reshape(128, 128) for n in range(4)]
        tiles = [t.reshape(16, 1, 8, 128) for t in swap_blocks(tiles)]
        block = jnp.concatenate(tiles, axis=1).reshape(512, 128)
        right[0, :, q * 128 : (q + 1) * 128] = block.astype(bf16)
    for n in range(8):
        tiles = landed[:, n].astype(f32)[:, :8].reshape(4, 4, 8, 128)
        tiles = swap_blocks([tiles[:, m].reshape(32, 128) for m in range(4)])
        for m in range(4):
            block = jnp.concatenate([t[m * 8 : (m + 1) * 8] for t in tiles], axis=0)
            left[n * 32 : (n + 1) * 32, m * 128 : (m + 1) * 128] = block.astype(bf16)

    swap = pltpu.make_async_remote_copy(
        src_ref=right.at[0], dst_ref=right.at[1], send_sem=dma.at[3], recv_sem=dma.at[4],
        device_id=(r, spot * 2 + 1 - core), device_id_type=MESH,
    )
    swap.start()

    def outward(R, C, half, send):
        return pltpu.make_async_remote_copy(
            src_ref=mixed.at[lax.rem(R, 8), half, lax.rem(C, 8)], dst_ref=back.at[r * 8 + spot],
            send_sem=dma.at[send], recv_sem=dma.at[6], device_id=(R, C), device_id_type=MESH,
        )

    for half in range(2):
        if half == 1:
            swap.wait()
        product = jnp.dot(left[...], right[half], preferred_element_type=f32)
        for q in range(2):
            tiles = product[:, q * 128 : (q + 1) * 128].reshape(8, 4, 8, 128)
            tiles = swap_blocks([tiles[:, m].reshape(64, 128) for m in range(4)])
            for m in range(4):
                mixed[:, half, q * 4 + m] = tiles[m].reshape(8, 8, 128).astype(bf16)
        X = lax.rem(core + half, 2)
        for t in range(8):
            def go_out(s, _, t=t, half=half, X=X):
                R = core * 8 + lax.rem(z + z_step(t), 8)
                C = X * 8 + lax.rem(y + y_step(lax.div(s, 2)), 4) * 2 + lax.rem(core + s, 2)
                outward(R, C, half, 5).start()
                return 0

            lax.fori_loop(0, 8 if t < 7 else 6, go_out, 0)
        R, C = core * 8 + z, X * 8 + y * 2
        outward(R, C + 1 - core, half, 5).start()
        mine = (xh == core) & (xl == X)
        own_out = pltpu.make_async_copy(
            mixed.at[z, half, lax.rem(c, 8)], back.at[r * 8 + spot], dma.at[6]
        )
        pl.when(mine)(own_out.start)
        pl.when(jnp.logical_not(mine))(outward(R, C + core, half, 7 + half).start)

    pltpu.make_async_copy(back, back, dma.at[6]).wait()

    def total(n, s):
        return s + jnp.sum(back[pl.ds(n * 16, 16)].astype(f32), axis=0)

    center = lax.fori_loop(0, 8, total, jnp.zeros((8, 128), f32)) / 128

    def square(n, s):
        x = back[pl.ds(n * 16, 16)].astype(f32) - center[None]
        return s + jnp.sum(x * x, axis=0)

    scale = lax.rsqrt(lax.fori_loop(0, 8, square, jnp.zeros((8, 128), f32)) / 128 + EPSILON)

    def rescale(n, _):
        x = (back[pl.ds(n * 16, 16)].astype(f32) - center[None]) * scale[None]
        staged[pl.ds(n * 128, 128), :] = x.reshape(128, 128)
        return 0

    lax.fori_loop(0, 8, rescale, 0)
    for s in range(8):
        x = staged[pl.ds(s, 128, stride=8), :] * gain[...] + bias[...]
        x = lax.dot_general(x.astype(bf16), out_weight[...], TN, preferred_element_type=f32)
        for b in range(4):
            out[b * 8 + s] = (gate[b * 8 + s] * x[b * 32 : (b + 1) * 32]).astype(bf16)

    left_over = sent.at[pl.ds(0, 127)]
    pltpu.make_async_copy(left_over, left_over, dma.at[0]).wait()
    pl.when(xl != core)(pltpu.make_async_copy(sent.at[0], sent.at[0], dma.at[2]).wait)
    left_over = back.at[pl.ds(0, 126)]
    pltpu.make_async_copy(left_over, left_over, dma.at[5]).wait()
    for half in range(2):
        mine = (xh == core) & (xl == lax.rem(core + half, 2))
        one = pltpu.make_async_copy(back.at[0], back.at[0], dma.at[7 + half])
        pl.when(jnp.logical_not(mine))(one.wait)


def local(pair, norm_in, shift_in, in_weight, norm_out, shift_out, out_weight):
    f32, bf16 = jnp.float32, jnp.bfloat16
    vmem = pl.BlockSpec(memory_space=pltpu.VMEM)
    return pl.pallas_call(
        kernel,
        out_shape=jax.ShapeDtypeStruct((32, 32, 128), bf16),
        in_specs=[vmem] * 7,
        out_specs=vmem,
        scratch_shapes=[
            pltpu.VMEM((32 * PITCH, 128), f32),
            pltpu.VMEM((2048, 128), f32),
            pltpu.VMEM((128, 16, 128), bf16),
            pltpu.VMEM((16, 8, 16, 128), bf16),
            pltpu.VMEM((256, 512), bf16),
            pltpu.VMEM((2, 512, 256), bf16),
            pltpu.VMEM((8, 2, 8, 8, 128), bf16),
            pltpu.VMEM((128, 8, 128), bf16),
            pltpu.VMEM((32, 32, 128), f32),
            pltpu.VMEM((128, 128), f32),
            pltpu.VMEM((128, 128), f32),
            pltpu.VMEM((512, 128), bf16),
            pltpu.SemaphoreType.DMA((9,)),
            pltpu.SemaphoreType.REGULAR,
        ],
        name="triangle",
        compiler_params=pltpu.CompilerParams(collective_id=0, has_side_effects=True),
    )(
        pair.reshape(1024, 128), norm_in.reshape(1, 128), shift_in.reshape(1, 128), in_weight,
        norm_out.reshape(1, 128), shift_out.reshape(1, 128), out_weight,
    )


def solution(mesh):
    in_specs = (P("row", "col", None), P(), P(), P(), P(), P(), P())
    out_specs = P("row", "col", None)
    return jax.shard_map(local, mesh=mesh, in_specs=in_specs, out_specs=out_specs, check_vma=False)
```

time: 180 us -> 43.3 us (0.24)
  waiting for transfers between devices: 97.8 us -> 0 us
  Pallas kernels: 0 us -> 41.5 us
  blocking collectives: 35.7 us -> 0 us
  local copies, waits for them, and re-layouts: 19.3 us -> 1.67 us
  between operations: 13.5 us -> 0.01 us
  matrix products: 6.37 us -> 0 us
  other arithmetic: 5.36 us -> 0 us
    all_gather x2 -> x0, waiting for transfers between devices: 97.8 us -> none  [the longest x1 63.6 us: local(): right_full = lax.all_gather(right, 'row', axis=0, tiled=True)]
    pallas_call x0 -> x1, Pallas kernels: none -> 41.5 us  [local(): pl.pallas_call(kernel, out_shape=jax.ShapeDtypeStruct((32, 32, 128), bf16...]
    all_to_all x2 -> x0, blocking collectives: 35.7 us -> none  [the longest x1 23.1 us: local(): lax.all_to_all(sorted_parts, 'row', split_axis=1, concat_axis=0, tiled=True)]
    all_gather x2 -> x0, local copies, waits for them, and re-layouts: 16.5 us -> none  [the longest x1 8.62 us: local(): right_full = lax.all_gather(right, 'row', axis=0, tiled=True)]
    dot_general x3 -> x0, matrix products: 6.37 us -> none  [the longest x1 4.72 us: local(): jnp.einsum('kih,kjh->ijh', lax.all_gather(own_parts, 'col', axis=1, tiled...]
    reduce_sum x3 -> x0, other arithmetic: 2.9 us -> none  [the longest x2 1.71 us: layer_norm(): spread = jnp.mean(jnp.square(values - center), axis=-1, keepdims=True)]
    convert_element_type x2 -> x0, other arithmetic: 2.43 us -> none  [the longest x1 1.31 us: local(): normed = layer_norm(pair, norm_in, shift_in).astype(jnp.bfloat16)]
  transfers between devices with their start and end apart: 2 -> 0, of which waited for: 2 -> 0; matrix products, arithmetic and copies ran while one was open for 6% -> 0% of each run, Pallas kernels for 0% -> 0%
where the time goes in v1:
time: 43.3 us; the launch traced here: 43.2 us
  Pallas kernels  41.5 us (96%)
  local copies, waits for them, and re-layouts  1.67 us (4%)
    pallas_call x1, Pallas kernels, local(): pl.pallas_call(kernel, out_shape=jax.ShapeDtypeStruct((32, 32, 128), bf16...  41.5 us
    unnamed x1, local copies, waits for them, and re-layouts  1.67 us

profile of v1, /device:TPU:3, one launch (start us, length us, event | category | flops | bytes accessed | tf_op | source)
XLA Modules:
  0.0 43.2 jit_solution(11732474993847713713)
XLA Ops:
  0.0 41.5 %triangle.1 = bf16[32,32,128]{2,1,0:T(8,128)(2,1)} custom-call(bf16[1024,128]{1,0:T(8,128)(2,1)} %bitcast.5, f32[1,128]{1,0:T(1,128)} %bitcast.6, f32[1,128]{1,0:T(1,128)} %bitcast.7, bf16[128,640]{1,0:T(8,128)(2,1)} %in_weight.1, f32[1,128]{1,0:T(1,128)} %bitcast.8, f32[1,128]{1,0:T(1,128)} %bitcast.9, bf16[128,128]{1,0:T(8,128)(2,1)} %out_weight.1), custom_call_target="tpu_custom_call" | custom-call | tf_op jit(solution)/shard_map/triangle/pallas_call | solution.py:214
  41.5 1.7 %copy.9 = bf16[32,32,128]{2,1,0:T(8,128)(2,1)} copy(bf16[32,32,128]{2,1,0:T(8,128)(2,1)} %triangle.1) | data formatting | bytes 524288

commit v2 on v1

--- a/solution.py
+++ b/solution.py
@@ -10,14 +10,15 @@
 PITCH = 40
 NT = (((1,), (1,)), ((), ()))
 TN = (((0,), (0,)), ((), ()))
+Y_STEP = (2, 1, 3, 0)
+ORDER = (
+    (0, 0), (0, 1), (0, 3), (1, 0), (3, 0), (0, 2), (1, 1), (1, 3),
+    (3, 1), (3, 3), (2, 0), (1, 2), (3, 2), (2, 1), (2, 3), (2, 2),
+)
 
 
 def z_step(t):
     return 4 + (1 - 2 * (t % 2)) * ((t + 1) // 2)
-
-
-def y_step(u):
-    return 2 + (1 - 2 * lax.rem(u, 2)) * lax.div(u + 1, 2)
 
 
 def swap_blocks(tiles):
@@ -36,9 +37,10 @@
 
 
 def kernel(
-    pair, norm_in, shift_in, in_weight, norm_out, shift_out, out_weight, out,
+    pair_in, norm_in_in, shift_in_in, in_weight_in, norm_out_in, shift_out_in, out_weight_in, out,
+    pair, norm_in, shift_in, in_weight, norm_out, shift_out, out_weight,
     normed, staged, sent, landed, left, right, mixed, back, gate, gain, bias, weight,
-    dma, ready,
+    dma, load, ready,
 ):
     f32, bf16 = jnp.float32, jnp.bfloat16
     r, c = lax.axis_index("row"), lax.axis_index("col")
@@ -46,11 +48,30 @@
     xl, y, core = lax.div(c, 8), lax.rem(lax.div(c, 2), 4), lax.rem(c, 2)
     spot = lax.div(c, 2)
 
+    sources = (pair_in, norm_in_in, shift_in_in, in_weight_in, norm_out_in, shift_out_in, out_weight_in)
+    places = (pair, norm_in, shift_in, in_weight, norm_out, shift_out, out_weight)
+    loads = [pltpu.make_async_copy(f, t, load.at[n]) for n, (f, t) in enumerate(zip(sources, places))]
+    for n in (0, 3, 1, 2, 4, 5, 6):
+        loads[n].start()
+
+    def line(dx, dy):
+        x = lax.rem(2 * xh + xl + dx, 4)
+        return lax.div(x, 2), lax.rem(x, 2) * 4 + lax.rem(y + dy, 4)
+
+    def tell(semaphore, R, C):
+        pl.semaphore_signal(semaphore, inc=1, device_id=(R, C), device_id_type=MESH)
+
     barrier = pltpu.get_barrier_semaphore()
-    for s in range(1, 16):
-        pl.semaphore_signal(barrier, inc=1, device_id=(lax.rem(r + s, 16), c), device_id_type=MESH)
-    for s in range(1, 16):
-        pl.semaphore_signal(barrier, inc=1, device_id=(r, lax.rem(c + s, 16)), device_id_type=MESH)
+    for dx, dy in ((1, 0), (3, 0), (0, 1), (0, 3)):
+        H, S = line(dx, dy)
+        tell(barrier, H * 8 + z, S * 2 + core)
+    for dz in (4, 3, 5, 2, 6, 1, 7):
+        for e in range(2):
+            tell(barrier, xh * 8 + lax.rem(z + dz, 8), spot * 2 + e)
+    tell(barrier, r, spot * 2 + 1 - core)
+
+    for n in (0, 1, 2):
+        loads[n].wait()
 
     def norm_rows(n, _):
         x = pair[pl.ds(n * 128, 128), :].astype(f32)
@@ -63,6 +84,7 @@
         return 0
 
     lax.fori_loop(0, 8, norm_rows, 0)
+    loads[3].wait()
     weight[...] = in_weight[:, :512].astype(f32).T.astype(bf16)
 
     def glu(rows, x):
@@ -85,28 +107,41 @@
 
     lax.fori_loop(0, 8, pack, 0)
 
-    pl.semaphore_wait(barrier, 30)
-    for s in range(1, 16):
-        pl.semaphore_signal(ready, inc=1, device_id=(r, lax.rem(c + s, 16)), device_id_type=MESH)
-    pl.semaphore_wait(ready, 15)
-
     def inward(R, S, send):
         return pltpu.make_async_remote_copy(
             src_ref=sent.at[R * 8 + S], dst_ref=landed.at[r, lax.rem(c, 8)], send_sem=dma.at[send],
             recv_sem=dma.at[1], device_id=(R, S * 2 + xl), device_id_type=MESH,
         )
 
-    for t in range(8):
-        def go_in(s, _, t=t):
-            R = lax.rem(xh + 1 - lax.div(s, 8), 2) * 8 + lax.rem(z + z_step(t), 8)
-            S = lax.rem(xl + 1 - lax.rem(lax.div(s, 4), 2), 2) * 4 + lax.rem(y + y_step(lax.rem(s, 4)), 4)
-            inward(R, S, 0).start()
+    pl.semaphore_wait(barrier, 19)
+    for dx, dy in ORDER:
+        H, S = line(dx, dy)
+        if (dx, dy) != (0, 0):
+            pl.semaphore_wait(ready.at[dx * 4 + dy], 1)
+
+        def pass_on(ex, ey, dx=dx, dy=dy):
+            h, s = line(ex, ey)
+            tell(ready.at[(dx - ex) % 4 * 4 + (dy - ey) % 4], h * 8 + z, s * 2 + core)
+
+        if dx == 0:
+            if dy in (0, 1):
+                pass_on(0, 3)
+            if dy == 0:
+                pass_on(0, 1)
+            pass_on(3, 0)
+            pass_on(1, 0)
+        if dx == 1:
+            pass_on(3, 0)
+
+        def go_in(t, _, H=H, S=S):
+            inward(H * 8 + lax.rem(z + z_step(t), 8), S, 0).start()
             return 0
 
-        lax.fori_loop(0, 16 if t < 7 else 15, go_in, 0)
-    own_in = pltpu.make_async_copy(sent.at[r * 8 + spot], landed.at[r, lax.rem(c, 8)], dma.at[1])
-    pl.when(xl == core)(own_in.start)
-    pl.when(xl != core)(inward(r, spot, 2).start)
+        lax.fori_loop(0, 7 if (dx, dy) == (0, 0) else 8, go_in, 0, unroll=True)
+        if (dx, dy) == (0, 0):
+            own_in = pltpu.make_async_copy(sent.at[r * 8 + spot], landed.at[r, lax.rem(c, 8)], dma.at[1])
+            pl.when(xl == core)(own_in.start)
+            pl.when(xl != core)(inward(r, spot, 2).start)
 
     def gate_rows(n, _):
         parts = [normed[pl.ds((n * 4 + m) * PITCH, 32), :] for m in range(4)]
@@ -116,6 +151,8 @@
         return 0
 
     lax.fori_loop(0, 8, gate_rows, 0)
+    for n in (4, 5, 6):
+        loads[n].wait()
     gain[...] = jnp.broadcast_to(norm_out[...], (128, 128)).T
     bias[...] = jnp.broadcast_to(shift_out[...], (128, 128)).T
 
@@ -155,15 +192,20 @@
             for m in range(4):
                 mixed[:, half, q * 4 + m] = tiles[m].reshape(8, 8, 128).astype(bf16)
         X = lax.rem(core + half, 2)
-        for t in range(8):
-            def go_out(s, _, t=t, half=half, X=X):
-                R = core * 8 + lax.rem(z + z_step(t), 8)
-                C = X * 8 + lax.rem(y + y_step(lax.div(s, 2)), 4) * 2 + lax.rem(core + s, 2)
-                outward(R, C, half, 5).start()
-                return 0
-
-            lax.fori_loop(0, 8 if t < 7 else 6, go_out, 0)
+
+        def go_out(t, _, half=half, X=X):
+            R = core * 8 + lax.rem(z + z_step(t), 8)
+            for u in range(4):
+                for e in range(2):
+                    C = X * 8 + lax.rem(y + Y_STEP[u], 4) * 2 + lax.rem(core + 1 - e, 2)
+                    outward(R, C, half, 5).start()
+            return 0
+
+        lax.fori_loop(0, 7, go_out, 0)
         R, C = core * 8 + z, X * 8 + y * 2
+        for u in range(3):
+            for e in range(2):
+                outward(R, X * 8 + lax.rem(y + Y_STEP[u], 4) * 2 + e, half, 5).start()
         outward(R, C + 1 - core, half, 5).start()
         mine = (xh == core) & (xl == X)
         own_out = pltpu.make_async_copy(
@@ -210,13 +252,21 @@
 
 def local(pair, norm_in, shift_in, in_weight, norm_out, shift_out, out_weight):
     f32, bf16 = jnp.float32, jnp.bfloat16
+    hbm = pl.BlockSpec(memory_space=pltpu.HBM)
     vmem = pl.BlockSpec(memory_space=pltpu.VMEM)
     return pl.pallas_call(
         kernel,
         out_shape=jax.ShapeDtypeStruct((32, 32, 128), bf16),
-        in_specs=[vmem] * 7,
+        in_specs=[hbm] * 7,
         out_specs=vmem,
         scratch_shapes=[
+            pltpu.VMEM((1024, 128), bf16),
+            pltpu.VMEM((1, 128), f32),
+            pltpu.VMEM((1, 128), f32),
+            pltpu.VMEM((128, 640), bf16),
+            pltpu.VMEM((1, 128), f32),
+            pltpu.VMEM((1, 128), f32),
+            pltpu.VMEM((128, 128), bf16),
             pltpu.VMEM((32 * PITCH, 128), f32),
             pltpu.VMEM((2048, 128), f32),
             pltpu.VMEM((128, 16, 128), bf16),
@@ -230,7 +280,8 @@
             pltpu.VMEM((128, 128), f32),
             pltpu.VMEM((512, 128), bf16),
             pltpu.SemaphoreType.DMA((9,)),
-            pltpu.SemaphoreType.REGULAR,
+            pltpu.SemaphoreType.DMA((7,)),
+            pltpu.SemaphoreType.REGULAR((16,)),
         ],
         name="triangle",
         compiler_params=pltpu.CompilerParams(collective_id=0, has_side_effects=True),

time: 43.3 us -> 40 us (0.924)
  Pallas kernels: 41.5 us -> 38.2 us
    pallas_call x1, Pallas kernels: 41.5 us -> 38.2 us  [local(): pl.pallas_call(kernel, out_shape=jax.ShapeDtypeStruct((32, 32, 128), bf16...]
where the time goes in v2:
time: 40 us; the launch traced here: 39.8 us
  Pallas kernels  38.2 us (96%)
  local copies, waits for them, and re-layouts  1.67 us (4%)
    pallas_call x1, Pallas kernels, local(): pl.pallas_call(kernel, out_shape=jax.ShapeDtypeStruct((32, 32, 128), bf16...  38.2 us
    unnamed x1, local copies, waits for them, and re-layouts  1.67 us

profile of v2, /device:TPU:3, one launch (start us, length us, event | category | flops | bytes accessed | tf_op | source)
XLA Modules:
  0.0 39.8 jit_solution(427724878680000726)
XLA Ops:
  0.0 38.2 %triangle.1 = bf16[32,32,128]{2,1,0:T(8,128)(2,1)} custom-call(bf16[1024,128]{1,0:T(8,128)(2,1)} %bitcast.5, f32[1,128]{1,0:T(1,128)} %bitcast.6, f32[1,128]{1,0:T(1,128)} %bitcast.7, bf16[128,640]{1,0:T(8,128)(2,1)} %in_weight_in.1, f32[1,128]{1,0:T(1,128)} %bitcast.8, f32[1,128]{1,0:T(1,128)} %bitcast.9, bf16[128,128]{1,0:T(8,128)(2,1)} %out_weight_in.1), custom_call_target="tpu_custom_call" | custom-call | tf_op jit(solution)/shard_map/triangle/pallas_call | solution.py:257
  38.2 1.7 %copy.9 = bf16[32,32,128]{2,1,0:T(8,128)(2,1)} copy(bf16[32,32,128]{2,1,0:T(8,128)(2,1)} %triangle.1) | data formatting | bytes 524288

commit v3 on v2

--- a/solution.py
+++ b/solution.py
@@ -15,6 +15,7 @@
     (0, 0), (0, 1), (0, 3), (1, 0), (3, 0), (0, 2), (1, 1), (1, 3),
     (3, 1), (3, 3), (2, 0), (1, 2), (3, 2), (2, 1), (2, 3), (2, 2),
 )
+LAST = ((1, 0), (3, 0), (0, 3))
 
 
 def z_step(t):
@@ -113,9 +114,21 @@
             recv_sem=dma.at[1], device_id=(R, S * 2 + xl), device_id_type=MESH,
         )
 
+    def send_line(dx, dy):
+        H, S = line(dx, dy)
+
+        def go_in(t, _):
+            inward(H * 8 + lax.rem(z + z_step(t), 8), S, 0).start()
+            return 0
+
+        lax.fori_loop(0, 7 if (dx, dy) == (0, 0) else 8, go_in, 0, unroll=True)
+        if (dx, dy) == (0, 0):
+            own_in = pltpu.make_async_copy(sent.at[r * 8 + spot], landed.at[r, lax.rem(c, 8)], dma.at[1])
+            pl.when(xl == core)(own_in.start)
+            pl.when(xl != core)(inward(r, spot, 2).start)
+
     pl.semaphore_wait(barrier, 19)
     for dx, dy in ORDER:
-        H, S = line(dx, dy)
         if (dx, dy) != (0, 0):
             pl.semaphore_wait(ready.at[dx * 4 + dy], 1)
 
@@ -133,15 +146,10 @@
         if dx == 1:
             pass_on(3, 0)
 
-        def go_in(t, _, H=H, S=S):
-            inward(H * 8 + lax.rem(z + z_step(t), 8), S, 0).start()
-            return 0
-
-        lax.fori_loop(0, 7 if (dx, dy) == (0, 0) else 8, go_in, 0, unroll=True)
-        if (dx, dy) == (0, 0):
-            own_in = pltpu.make_async_copy(sent.at[r * 8 + spot], landed.at[r, lax.rem(c, 8)], dma.at[1])
-            pl.when(xl == core)(own_in.start)
-            pl.when(xl != core)(inward(r, spot, 2).start)
+        if (dx, dy) not in LAST:
+            send_line(dx, dy)
+    for dx, dy in LAST:
+        send_line(dx, dy)
 
     def gate_rows(n, _):
         parts = [normed[pl.ds((n * 4 + m) * PITCH, 32), :] for m in range(4)]
@@ -193,19 +201,17 @@
                 mixed[:, half, q * 4 + m] = tiles[m].reshape(8, 8, 128).astype(bf16)
         X = lax.rem(core + half, 2)
 
-        def go_out(t, _, half=half, X=X):
-            R = core * 8 + lax.rem(z + z_step(t), 8)
-            for u in range(4):
+        for u in range(4):
+            far = X * 8 + lax.rem(y + Y_STEP[u], 4) * 2
+
+            def go_out(t, _, half=half, far=far):
+                R = core * 8 + lax.rem(z + z_step(t), 8)
                 for e in range(2):
-                    C = X * 8 + lax.rem(y + Y_STEP[u], 4) * 2 + lax.rem(core + 1 - e, 2)
-                    outward(R, C, half, 5).start()
-            return 0
-
-        lax.fori_loop(0, 7, go_out, 0)
+                    outward(R, far + e, half, 5).start()
+                return 0
+
+            lax.fori_loop(0, 7 if u == 3 else 8, go_out, 0, unroll=True)
         R, C = core * 8 + z, X * 8 + y * 2
-        for u in range(3):
-            for e in range(2):
-                outward(R, X * 8 + lax.rem(y + Y_STEP[u], 4) * 2 + e, half, 5).start()
         outward(R, C + 1 - core, half, 5).start()
         mine = (xh == core) & (xl == X)
         own_out = pltpu.make_async_copy(
@@ -256,7 +262,7 @@
     vmem = pl.BlockSpec(memory_space=pltpu.VMEM)
     return pl.pallas_call(
         kernel,
-        out_shape=jax.ShapeDtypeStruct((32, 32, 128), bf16),
+        out_shape=pltpu.VMEM((32, 32, 128), bf16),
         in_specs=[hbm] * 7,
         out_specs=vmem,
         scratch_shapes=[

time: 40 us -> 37.1 us (0.927)
  Pallas kernels: 38.2 us -> 36.3 us
  local copies, waits for them, and re-layouts: 1.67 us -> 0.71 us
    pallas_call x1, Pallas kernels: 38.2 us -> 36.3 us  [local(): pl.pallas_call(kernel, out_shape=pltpu.VMEM((32, 32, 128), bf16), in_spec...]
    unnamed x1, local copies, waits for them, and re-layouts: 1.67 us -> 0.71 us
where the time goes in v3:
time: 37.1 us; the launch traced here: 37 us
  Pallas kernels  36.3 us (98%)
  local copies, waits for them, and re-layouts  0.71 us (2%)
    pallas_call x1, Pallas kernels, local(): pl.pallas_call(kernel, out_shape=pltpu.VMEM((32, 32, 128), bf16), in_spec...  36.3 us

profile of v3, /device:TPU:3, one launch (start us, length us, event | category | flops | bytes accessed | tf_op | source)
XLA Modules:
  0.0 37.0 jit_solution(16242219739527792983)
XLA Ops:
  0.0 36.3 %triangle.1 = bf16[32,32,128]{2,1,0:T(8,128)(2,1)S(1)} custom-call(bf16[1024,128]{1,0:T(8,128)(2,1)} %bitcast.5, f32[1,128]{1,0:T(1,128)} %bitcast.6, f32[1,128]{1,0:T(1,128)} %bitcast.7, bf16[128,640]{1,0:T(8,128)(2,1)} %in_weight_in.1, f32[1,128]{1,0:T(1,128)} %bitcast.8, f32[1,128]{1,0:T(1,128)} %bitcast.9, bf16[128,128]{1,0:T(8,128)(2,1)} %out_weight_in.1), custom_call_target="tpu_custom_call" | custom-call | tf_op jit(solution)/shard_map/triangle/pallas_call | solution.py:263
  36.3 0.7 %copy.9 = bf16[32,32,128]{2,1,0:T(8,128)(2,1)} copy(bf16[32,32,128]{2,1,0:T(8,128)(2,1)S(1)} %triangle.1) | data formatting | bytes 524288

commit v4 on v3

--- a/solution.py
+++ b/solution.py
@@ -108,10 +108,12 @@
 
     lax.fori_loop(0, 8, pack, 0)
 
+    arrived = dma.at[1 + 8 * lax.div(y, 2)]
+
     def inward(R, S, send):
         return pltpu.make_async_remote_copy(
             src_ref=sent.at[R * 8 + S], dst_ref=landed.at[r, lax.rem(c, 8)], send_sem=dma.at[send],
-            recv_sem=dma.at[1], device_id=(R, S * 2 + xl), device_id_type=MESH,
+            recv_sem=arrived, device_id=(R, S * 2 + xl), device_id_type=MESH,
         )
 
     def send_line(dx, dy):
@@ -123,7 +125,7 @@
 
         lax.fori_loop(0, 7 if (dx, dy) == (0, 0) else 8, go_in, 0, unroll=True)
         if (dx, dy) == (0, 0):
-            own_in = pltpu.make_async_copy(sent.at[r * 8 + spot], landed.at[r, lax.rem(c, 8)], dma.at[1])
+            own_in = pltpu.make_async_copy(sent.at[r * 8 + spot], landed.at[r, lax.rem(c, 8)], arrived)
             pl.when(xl == core)(own_in.start)
             pl.when(xl != core)(inward(r, spot, 2).start)
 
@@ -164,61 +166,53 @@
     gain[...] = jnp.broadcast_to(norm_out[...], (128, 128)).T
     bias[...] = jnp.broadcast_to(shift_out[...], (128, 128)).T
 
-    pltpu.make_async_copy(landed, landed, dma.at[1]).wait()
+    def swap(q):
+        return pltpu.make_async_remote_copy(
+            src_ref=right.at[0, q], dst_ref=right.at[1, q], send_sem=dma.at[3 + 4 * q], recv_sem=dma.at[4 + 4 * q],
+            device_id=(r, spot * 2 + 1 - core), device_id_type=MESH,
+        )
+
+    def outward(R, C, half):
+        return pltpu.make_async_remote_copy(
+            src_ref=mixed.at[lax.rem(R, 8), half, lax.rem(C, 8)], dst_ref=back.at[r * 8 + spot],
+            send_sem=dma.at[5], recv_sem=dma.at[6], device_id=(R, C), device_id_type=MESH,
+        )
+
+    def answer(half, g, q):
+        product = jnp.dot(left[g * 128 : (g + 1) * 128], right[half, q], preferred_element_type=f32)
+        tiles = product.reshape(4, 4, 8, 128)
+        tiles = swap_blocks([tiles[:, m].reshape(32, 128) for m in range(4)])
+        for m in range(4):
+            mixed[g * 4 : (g + 1) * 4, half, q * 4 + m] = tiles[m].reshape(4, 8, 128).astype(bf16)
+        X = lax.rem(core + half, 2)
+        for db in (2, 3, 1, 0):
+            C = X * 8 + q * 4 + lax.rem(c + db, 4)
+            for da in (2, 1, 3, 0):
+                R = core * 8 + g * 4 + lax.rem(z + da, 4)
+                if da or db:
+                    outward(R, C, half).start()
+        mine = (xh == core) & (xl == X) & (lax.div(z, 4) == g) & (lax.div(y, 2) == q)
+        own_out = pltpu.make_async_copy(mixed.at[z, half, lax.rem(c, 8)], back.at[r * 8 + spot], dma.at[6])
+        pl.when(mine)(own_out.start)
+        pl.when(jnp.logical_not(mine))(outward(R, C, half).start)
 
     for q in range(2):
+        pltpu.make_async_copy(landed.at[0:8], landed.at[0:8], dma.at[1 + 8 * q]).wait()
         tiles = [landed[:, q * 4 + n].astype(f32)[:, 8:].reshape(128, 128) for n in range(4)]
         tiles = [t.reshape(16, 1, 8, 128) for t in swap_blocks(tiles)]
-        block = jnp.concatenate(tiles, axis=1).reshape(512, 128)
-        right[0, :, q * 128 : (q + 1) * 128] = block.astype(bf16)
-    for n in range(8):
-        tiles = landed[:, n].astype(f32)[:, :8].reshape(4, 4, 8, 128)
-        tiles = swap_blocks([tiles[:, m].reshape(32, 128) for m in range(4)])
-        for m in range(4):
-            block = jnp.concatenate([t[m * 8 : (m + 1) * 8] for t in tiles], axis=0)
-            left[n * 32 : (n + 1) * 32, m * 128 : (m + 1) * 128] = block.astype(bf16)
-
-    swap = pltpu.make_async_remote_copy(
-        src_ref=right.at[0], dst_ref=right.at[1], send_sem=dma.at[3], recv_sem=dma.at[4],
-        device_id=(r, spot * 2 + 1 - core), device_id_type=MESH,
-    )
-    swap.start()
-
-    def outward(R, C, half, send):
-        return pltpu.make_async_remote_copy(
-            src_ref=mixed.at[lax.rem(R, 8), half, lax.rem(C, 8)], dst_ref=back.at[r * 8 + spot],
-            send_sem=dma.at[send], recv_sem=dma.at[6], device_id=(R, C), device_id_type=MESH,
-        )
-
-    for half in range(2):
-        if half == 1:
-            swap.wait()
-        product = jnp.dot(left[...], right[half], preferred_element_type=f32)
-        for q in range(2):
-            tiles = product[:, q * 128 : (q + 1) * 128].reshape(8, 4, 8, 128)
-            tiles = swap_blocks([tiles[:, m].reshape(64, 128) for m in range(4)])
+        right[0, q] = jnp.concatenate(tiles, axis=1).reshape(512, 128).astype(bf16)
+        for n in range(q * 4, q * 4 + 4):
+            tiles = landed[:, n].astype(f32)[:, :8].reshape(4, 4, 8, 128)
+            tiles = swap_blocks([tiles[:, m].reshape(32, 128) for m in range(4)])
             for m in range(4):
-                mixed[:, half, q * 4 + m] = tiles[m].reshape(8, 8, 128).astype(bf16)
-        X = lax.rem(core + half, 2)
-
-        for u in range(4):
-            far = X * 8 + lax.rem(y + Y_STEP[u], 4) * 2
-
-            def go_out(t, _, half=half, far=far):
-                R = core * 8 + lax.rem(z + z_step(t), 8)
-                for e in range(2):
-                    outward(R, far + e, half, 5).start()
-                return 0
-
-            lax.fori_loop(0, 7 if u == 3 else 8, go_out, 0, unroll=True)
-        R, C = core * 8 + z, X * 8 + y * 2
-        outward(R, C + 1 - core, half, 5).start()
-        mine = (xh == core) & (xl == X)
-        own_out = pltpu.make_async_copy(
-            mixed.at[z, half, lax.rem(c, 8)], back.at[r * 8 + spot], dma.at[6]
-        )
-        pl.when(mine)(own_out.start)
-        pl.when(jnp.logical_not(mine))(outward(R, C + core, half, 7 + half).start)
+                block = jnp.concatenate([t[m * 8 : (m + 1) * 8] for t in tiles], axis=0)
+                left[n * 32 : (n + 1) * 32, m * 128 : (m + 1) * 128] = block.astype(bf16)
+        swap(q).start()
+        for half in range(2):
+            if half == 1:
+                swap(q).wait()
+            for place in ((0, 0),) if q == 0 else ((0, 1), (1, 0), (1, 1)):
+                answer(half, *place)
 
     pltpu.make_async_copy(back, back, dma.at[6]).wait()
 
@@ -248,12 +242,9 @@
     left_over = sent.at[pl.ds(0, 127)]
     pltpu.make_async_copy(left_over, left_over, dma.at[0]).wait()
     pl.when(xl != core)(pltpu.make_async_copy(sent.at[0], sent.at[0], dma.at[2]).wait)
-    left_over = back.at[pl.ds(0, 126)]
-    pltpu.make_async_copy(left_over, left_over, dma.at[5]).wait()
-    for half in range(2):
-        mine = (xh == core) & (xl == lax.rem(core + half, 2))
-        one = pltpu.make_async_copy(back.at[0], back.at[0], dma.at[7 + half])
-        pl.when(jnp.logical_not(mine))(one.wait)
+    left_over = back.at[pl.ds(0, 127)]
+    pl.when(xh == core)(pltpu.make_async_copy(left_over, left_over, dma.at[5]).wait)
+    pl.when(xh != core)(pltpu.make_async_copy(back, back, dma.at[5]).wait)
 
 
 def local(pair, norm_in, shift_in, in_weight, norm_out, shift_out, out_weight):
@@ -278,14 +269,14 @@
             pltpu.VMEM((128, 16, 128), bf16),
             pltpu.VMEM((16, 8, 16, 128), bf16),
             pltpu.VMEM((256, 512), bf16),
-            pltpu.VMEM((2, 512, 256), bf16),
+            pltpu.VMEM((2, 2, 512, 128), bf16),
             pltpu.VMEM((8, 2, 8, 8, 128), bf16),
             pltpu.VMEM((128, 8, 128), bf16),
             pltpu.VMEM((32, 32, 128), f32),
             pltpu.VMEM((128, 128), f32),
             pltpu.VMEM((128, 128), f32),
             pltpu.VMEM((512, 128), bf16),
-            pltpu.SemaphoreType.DMA((9,)),
+            pltpu.SemaphoreType.DMA((10,)),
             pltpu.SemaphoreType.DMA((7,)),
             pltpu.SemaphoreType.REGULAR((16,)),
         ],

time: 37.1 us -> 36.3 us (0.978)
  Pallas kernels: 36.3 us -> 35.2 us
    pallas_call x1, Pallas kernels: 36.3 us -> 35.2 us  [local(): pl.pallas_call(kernel, out_shape=pltpu.VMEM((32, 32, 128), bf16), in_spec...]
where the time goes in v4:
time: 36.3 us; the launch traced here: 35.9 us
  Pallas kernels  35.2 us (97%)
  local copies, waits for them, and re-layouts  0.71 us (2%)
    pallas_call x1, Pallas kernels, local(): pl.pallas_call(kernel, out_shape=pltpu.VMEM((32, 32, 128), bf16), in_spec...  35.2 us

profile of v4, /device:TPU:3, one launch (start us, length us, event | category | flops | bytes accessed | tf_op | source)
XLA Modules:
  0.0 35.9 jit_solution(1826885650488801336)
XLA Ops:
  0.0 35.2 %triangle.1 = bf16[32,32,128]{2,1,0:T(8,128)(2,1)S(1)} custom-call(bf16[1024,128]{1,0:T(8,128)(2,1)} %bitcast.5, f32[1,128]{1,0:T(1,128)} %bitcast.6, f32[1,128]{1,0:T(1,128)} %bitcast.7, bf16[128,640]{1,0:T(8,128)(2,1)} %in_weight_in.1, f32[1,128]{1,0:T(1,128)} %bitcast.8, f32[1,128]{1,0:T(1,128)} %bitcast.9, bf16[128,128]{1,0:T(8,128)(2,1)} %out_weight_in.1), custom_call_target="tpu_custom_call" | custom-call | tf_op jit(solution)/shard_map/triangle/pallas_call | solution.py:254
  35.2 0.7 %copy.9 = bf16[32,32,128]{2,1,0:T(8,128)(2,1)} copy(bf16[32,32,128]{2,1,0:T(8,128)(2,1)S(1)} %triangle.1) | data formatting | bytes 524288

commit v5 on v4

--- a/solution.py
+++ b/solution.py
@@ -52,7 +52,7 @@
     sources = (pair_in, norm_in_in, shift_in_in, in_weight_in, norm_out_in, shift_out_in, out_weight_in)
     places = (pair, norm_in, shift_in, in_weight, norm_out, shift_out, out_weight)
     loads = [pltpu.make_async_copy(f, t, load.at[n]) for n, (f, t) in enumerate(zip(sources, places))]
-    for n in (0, 3, 1, 2, 4, 5, 6):
+    for n in (3, 0, 1, 2, 4, 5, 6):
         loads[n].start()
 
     def line(dx, dy):
@@ -71,6 +71,8 @@
             tell(barrier, xh * 8 + lax.rem(z + dz, 8), spot * 2 + e)
     tell(barrier, r, spot * 2 + 1 - core)
 
+    loads[3].wait()
+    weight[...] = in_weight[:, :512].astype(f32).T.astype(bf16)
     for n in (0, 1, 2):
         loads[n].wait()
 
@@ -84,9 +86,7 @@
             normed[pl.ds((n * 4 + m) * PITCH, 32), :] = x[m * 32 : (m + 1) * 32]
         return 0
 
-    lax.fori_loop(0, 8, norm_rows, 0)
-    loads[3].wait()
-    weight[...] = in_weight[:, :512].astype(f32).T.astype(bf16)
+    lax.fori_loop(0, 8, norm_rows, 0, unroll=2)
 
     def glu(rows, x):
         p = lax.dot_general(weight[pl.ds(rows, 256), :], x, NT, preferred_element_type=f32)
@@ -106,7 +106,7 @@
         sent[pl.ds(n * 16, 16)] = staged[pl.ds(n * 256, 256), :].astype(bf16).reshape(16, 16, 128)
         return 0
 
-    lax.fori_loop(0, 8, pack, 0)
+    lax.fori_loop(0, 8, pack, 0, unroll=4)
 
     arrived = dma.at[1 + 8 * lax.div(y, 2)]
 
@@ -219,20 +219,20 @@
     def total(n, s):
         return s + jnp.sum(back[pl.ds(n * 16, 16)].astype(f32), axis=0)
 
-    center = lax.fori_loop(0, 8, total, jnp.zeros((8, 128), f32)) / 128
+    center = lax.fori_loop(0, 8, total, jnp.zeros((8, 128), f32), unroll=4) / 128
 
     def square(n, s):
         x = back[pl.ds(n * 16, 16)].astype(f32) - center[None]
         return s + jnp.sum(x * x, axis=0)
 
-    scale = lax.rsqrt(lax.fori_loop(0, 8, square, jnp.zeros((8, 128), f32)) / 128 + EPSILON)
+    scale = lax.rsqrt(lax.fori_loop(0, 8, square, jnp.zeros((8, 128), f32), unroll=4) / 128 + EPSILON)
 
     def rescale(n, _):
         x = (back[pl.ds(n * 16, 16)].astype(f32) - center[None]) * scale[None]
         staged[pl.ds(n * 128, 128), :] = x.reshape(128, 128)
         return 0
 
-    lax.fori_loop(0, 8, rescale, 0)
+    lax.fori_loop(0, 8, rescale, 0, unroll=4)
     for s in range(8):
         x = staged[pl.ds(s, 128, stride=8), :] * gain[...] + bias[...]
         x = lax.dot_general(x.astype(bf16), out_weight[...], TN, preferred_element_type=f32)
@@ -264,8 +264,8 @@
             pltpu.VMEM((1, 128), f32),
             pltpu.VMEM((1, 128), f32),
             pltpu.VMEM((128, 128), bf16),
-            pltpu.VMEM((32 * PITCH, 128), f32),
-            pltpu.VMEM((2048, 128), f32),
+            pltpu.VMEM((33 * PITCH, 128), f32),
+            pltpu.VMEM((2064, 128), f32),
             pltpu.VMEM((128, 16, 128), bf16),
             pltpu.VMEM((16, 8, 16, 128), bf16),
             pltpu.VMEM((256, 512), bf16),

time: 36.3 us -> 36.4 us (level)
  the two profiles are of different devices: /device:TPU:3 before, /device:TPU:19 now
where the time goes in v5:
time: 36.4 us; the launch traced here: 36.3 us
  Pallas kernels  35.6 us (98%)
  local copies, waits for them, and re-layouts  0.71 us (2%)
    pallas_call x1, Pallas kernels, local(): pl.pallas_call(kernel, out_shape=pltpu.VMEM((32, 32, 128), bf16), in_spec...  35.6 us

profile of v5, /device:TPU:19, one launch (start us, length us, event | category | flops | bytes accessed | tf_op | source)
XLA Modules:
  0.0 36.3 jit_solution(15854674289799101468)
XLA Ops:
  0.0 35.6 %triangle.1 = bf16[32,32,128]{2,1,0:T(8,128)(2,1)S(1)} custom-call(bf16[1024,128]{1,0:T(8,128)(2,1)} %bitcast.5, f32[1,128]{1,0:T(1,128)} %bitcast.6, f32[1,128]{1,0:T(1,128)} %bitcast.7, bf16[128,640]{1,0:T(8,128)(2,1)} %in_weight_in.1, f32[1,128]{1,0:T(1,128)} %bitcast.8, f32[1,128]{1,0:T(1,128)} %bitcast.9, bf16[128,128]{1,0:T(8,128)(2,1)} %out_weight_in.1), custom_call_target="tpu_custom_call" | custom-call | tf_op jit(solution)/shard_map/triangle/pallas_call | solution.py:254
  35.6 0.7 %copy.9 = bf16[32,32,128]{2,1,0:T(8,128)(2,1)} copy(bf16[32,32,128]{2,1,0:T(8,128)(2,1)S(1)} %triangle.1) | data formatting | bytes 524288
